TPU v7x, 128 devices: a whole 4x4x4 slice. The times are simulated.
128 devices in a mesh: batch: 32 (over z, x, core), cols: 4 (over y).
Axes of the slice: x: 4, y: 4, z: 4, core: 2. Of those that a mesh axis runs over, the one named last changes fastest.
Arguments:
- partial_query: float32 [32, 1024, 1024], P('batch', None, 'cols'), may hold values from -1.25 to 1.25
- partial_key: float32 [32, 1024, 1024], P('batch', None, 'cols'), may hold values from -1.25 to 1.25
- partial_value: float32 [32, 1024, 1024], P('batch', None, 'cols'), may hold values from -1.25 to 1.25
- partial_mixed: float32 [32, 1024, 1024], P('batch', 'cols'), may hold values from -1.25 to 1.25
- partial_norm: float32 [32, 1024], P('batch'), may hold values from -12 to 12
- partial_bias: float32 [32, 1024], P('batch'), may hold values from -12 to 12
- master_query: float32 [1024, 1024], P('batch', 'cols'), may hold values from -0.1875 to 0.1875
- master_key: float32 [1024, 1024], P('batch', 'cols'), may hold values from -0.1875 to 0.1875
- master_value: float32 [1024, 1024], P('batch', 'cols'), may hold values from -0.1875 to 0.1875
- master_mixed: float32 [1024, 1024], P('cols', 'batch'), may hold values from -0.1875 to 0.1875
- master_norm: float32 [1024], P('batch'), may hold values from 0.25 to 1.75
- master_bias: float32 [1024], P('batch'), may hold values from -3 to 3
Outputs:
- compute_query: bfloat16 [1024, 1024], P(None, 'cols')
- compute_key: bfloat16 [1024, 1024], P(None, 'cols')
- compute_value: bfloat16 [1024, 1024], P(None, 'cols')
- compute_mixed: bfloat16 [1024, 1024], P('cols')
- compute_norm: bfloat16 [1024], replicated
- compute_bias: bfloat16 [1024], replicated
- stepped_query: float32 [1024, 1024], P('batch', 'cols')
- stepped_key: float32 [1024, 1024], P('batch', 'cols')
- stepped_value: float32 [1024, 1024], P('batch', 'cols')
- stepped_mixed: float32 [1024, 1024], P('cols', 'batch')
- stepped_norm: float32 [1024], P('batch')
- stepped_bias: float32 [1024], P('batch')
All inputs are finite; a program needn't handle non-finite values.
Results may differ from a plain program's by a relative error of at most 0.001.
Values may be sent and summed in bfloat16 or wider, within the bound.
A program may use at most 64 MiB of HBM per device.

v0:
```python
import jax
import jax.numpy as jnp
from jax import lax
from jax.sharding import Mesh
from jax.sharding import PartitionSpec as P

BATCH = ("batch_0", "batch_1", "batch_2")


learn_rate = 0.4


def in_blocks(x, dim, count):
    shape = x.shape
    tiles = x.reshape(*shape[:dim], count, shape[dim] // count, *shape[dim + 1 :])
    return jnp.moveaxis(tiles, dim, 0)


def sent_and_summed(x, axis, dim):
    count = lax.axis_size(axis)
    tiles = lax.all_to_all(in_blocks(x, dim, count), axis, 0, 0, tiled=True)
    return jnp.sum(tiles, axis=0)


def sum_by_axis(x, axes, dim):
    far, near = axes
    own = sent_and_summed(in_blocks(x, dim, lax.axis_size(far)), near, dim + 1)
    return jnp.sum(lax.all_to_all(own, far, 0, 0, tiled=True), axis=0)


def side_by_side(arrays, axis, dim, along):
    ends, at = ([], 0)
    for a in arrays[:-1]:
        at += a.shape[along]
        ends.append(at)
    both = jnp.concatenate(arrays, axis=along)
    return tuple(jnp.split(sum_by_axis(both, axis, dim), ends, axis=along))


def gather_turned(arrays, axis, dims):
    turned = [jnp.moveaxis(a, dim, 0) for a, dim in zip(arrays, dims)]
    both = jnp.concatenate([t.reshape(len(t), -1) for t in turned], axis=1)
    whole, at, done = (lax.all_gather(both, axis, axis=0, tiled=True), 0, [])
    for t, dim in zip(turned, dims):
        share = whole[:, at : at + t[0].size].reshape(-1, *t.shape[1:])
        done.append(jnp.moveaxis(share, 0, dim))
        at += t[0].size
    return tuple(done)


def per_device(
    partial_query,
    partial_key,
    partial_value,
    partial_mixed,
    partial_norm,
    partial_bias,
    master_query,
    master_key,
    master_value,
    master_mixed,
    master_norm,
    master_bias,
):
    mean_query, mean_key, mean_value, mean_mixed, mean_norm, mean_bias = (
        *side_by_side(
            (partial_query[0], partial_key[0], partial_value[0]),
            (("batch_0", "batch_1"), "batch_2"),
            0,
            1,
        ),
        sum_by_axis(partial_mixed[0], (("batch_0", "batch_1"), "batch_2"), 1),
        sum_by_axis(partial_norm[0], (("batch_0", "batch_1"), "batch_2"), 0),
        sum_by_axis(partial_bias[0], (("batch_0", "batch_1"), "batch_2"), 0),
    )
    mean_rate = lax.axis_size(BATCH) ** (-0.5)
    mean_query = mean_query * mean_rate
    mean_key = mean_key * mean_rate
    mean_value = mean_value * mean_rate
    mean_mixed = mean_mixed * mean_rate
    mean_norm = mean_norm * mean_rate
    mean_bias = mean_bias * mean_rate
    stepped_query = master_query - learn_rate * mean_query
    stepped_key = master_key - learn_rate * mean_key
    stepped_value = master_value - learn_rate * mean_value
    stepped_mixed = master_mixed - learn_rate * mean_mixed
    stepped_norm = master_norm - learn_rate * mean_norm
    stepped_bias = master_bias - learn_rate * mean_bias
    compute_query, compute_key, compute_value, compute_mixed, compute_norm, compute_bias = (
        gather_turned(
            (
                stepped_query.astype(jnp.bfloat16),
                stepped_key.astype(jnp.bfloat16),
                stepped_value.astype(jnp.bfloat16),
                stepped_mixed.astype(jnp.bfloat16),
                stepped_norm.astype(jnp.bfloat16),
                stepped_bias.astype(jnp.bfloat16),
            ),
            BATCH,
            (0, 0, 0, 1, 0, 0),
        )
    )
    return (
        compute_query,
        compute_key,
        compute_value,
        compute_mixed,
        compute_norm,
        compute_bias,
        stepped_query,
        stepped_key,
        stepped_value,
        stepped_mixed,
        stepped_norm,
        stepped_bias,
    )


def solution(mesh):
    split = Mesh(
        mesh.devices.reshape(4, 4, 2, mesh.shape["cols"]), ("batch_0", "batch_1", "batch_2", "cols")
    )
    in_specs = (
        P(BATCH, None, "cols"),
        P(BATCH, None, "cols"),
        P(BATCH, None, "cols"),
        P(BATCH, "cols", None),
        P(BATCH, None),
        P(BATCH, None),
        P(BATCH, "cols"),
        P(BATCH, "cols"),
        P(BATCH, "cols"),
        P("cols", BATCH),
        P(BATCH),
        P(BATCH),
    )
    out_specs = (
        P(None, "cols"),
        P(None, "cols"),
        P(None, "cols"),
        P("cols", None),
        P(),
        P(),
        P(BATCH, "cols"),
        P(BATCH, "cols"),
        P(BATCH, "cols"),
        P("cols", BATCH),
        P(BATCH),
        P(BATCH),
    )
    return jax.shard_map(
        per_device, mesh=split, in_specs=in_specs, out_specs=out_specs, check_vma=False
    )
```

profile of v0, /device:TPU:1, one launch (start us, length us, event | category | flops | bytes accessed | tf_op | source)
XLA Modules:
  0.0 161.0 jit_solution(4723989277255362857)
XLA Ops:
  7.2 0.5 broadcast.18
  7.7 1.3 reduce.12
  9.0 0.1 reshape_reshape_squeeze.6
  9.1 0.7 reshape.72
  9.8 4.6 %all-to-all-start.4 = ((f32[2,1,512]{2,1,0:T(1,128)}), f32[2,1,512]{2,1,0:T(1,128)S(1)}, u32[]{:S(2)}, u32[]{:S(2)}) async-start(f32[2,1,512]{2,1,0:T(1,128)} %reshape.72), calls=%async_computation.4 | async-start | bytes 8192 | tf_op jit(solution)/shard_map/all_to_all | solution.py:21
  14.4 2.2 %maximum_bitcast_fusion = f32[2,16,32,768]{3,2,0,1:T(8,128)S(1)} fusion(f32[16,2,32,256]{3,2,1,0:T(8,128)} %bitcast.25, f32[16,2,32,256]{3,2,1,0:T(8,128)} %bitcast.26, f32[16,2,32,256]{3,2,1,0:T(8,128)} %bitcast.27), kind=kLoop, calls=%fused_computation | loop fusion | flops 1572864 | bytes 6291456 | tf_op jit(solution)/shard_map/transpose | solution.py:16
  16.6 2.0 %copy.46 = f32[2,16,32,768]{3,2,1,0:T(8,128)} copy(f32[2,16,32,768]{3,2,0,1:T(8,128)S(1)} %maximum_bitcast_fusion) | data formatting | bytes 6291456 | tf_op jit(solution)/shard_map/transpose | solution.py:16
  18.6 4.1 %all-to-all-start = ((f32[2,16,32,768]{3,2,1,0:T(8,128)}), f32[2,16,32,768]{3,2,1,0:T(8,128)S(1)}, u32[]{:S(2)}, u32[]{:S(2)}) async-start(f32[2,16,32,768]{3,2,1,0:T(8,128)} %copy.46), calls=%async_computation | async-start | bytes 6291456 | tf_op jit(solution)/shard_map/all_to_all | solution.py:21
  22.7 0.5 broadcast.20
  23.2 0.7 reduce.14
  23.9 0.1 reshape.73
  24.0 0.7 reduce.13
  24.6 0.1 reshape_reshape_squeeze.7
  24.7 0.1 reshape.74
  24.8 2.5 %copy.47 = f32[1,256,1024]{1,2,0:T(8,128)} copy(f32[1,256,1024]{2,1,0:T(8,128)} %param.15) | data formatting | bytes 2097152 | tf_op args[3]
  27.3 2.3 %copy.48 = f32[2,16,256,32]{2,3,1,0:T(8,128)} copy(f32[2,16,256,32]{2,3,0,1:T(8,128)} %bitcast.24) | data formatting | bytes 2097152 | tf_op jit(solution)/shard_map/transpose | solution.py:16
  29.7 0.6 reduce_sum.76
  30.3 3.4 %all_to_all.48 = f32[2,1,512]{2,1,0:T(1,128)S(1)} all-to-all(f32[2,1,512]{2,1,0:T(1,128)S(1)} %reshape.74), channel_id=1, replica_groups=mesh['batch_0'=4,'batch_1'=4,'batch_2'=2,'cols'=4] {'batch_2'}, dimensions={0} | all-to-all | bytes 8192 | tf_op jit(solution)/shard_map/all_to_all | solution.py:21
  33.6 6.5 %all_to_all.49 = f32[2,16,256,32]{2,3,1,0:T(8,128)} all-to-all(f32[2,16,256,32]{2,3,1,0:T(8,128)} %copy.48), channel_id=1, replica_groups=mesh['batch_0'=4,'batch_1'=4,'batch_2'=2,'cols'=4] {'batch_2'}, dimensions={0} | all-to-all | bytes 2097152 | tf_op jit(solution)/shard_map/all_to_all | solution.py:21
  40.2 7.7 %all-to-all-start.5 = ((f32[16,1,32]{2,1,0:T(1,128)}), f32[16,1,32]{2,1,0:T(1,128)S(1)}, u32[]{:S(2)}, u32[]{:S(2)}) async-start(f32[16,1,32]{2,1,0:T(1,128)} %bitcast.10), calls=%async_computation.5 | async-start | bytes 16384 | tf_op jit(solution)/shard_map/all_to_all | solution.py:28
  47.9 0.7 reduce.15
  48.6 0.1 reshape.75
  48.6 0.6 reduce_sum.78
  49.3 5.0 %all-to-all-done.5 = f32[16,1,32]{2,1,0:T(1,128)S(1)} async-done(((f32[16,1,32]{2,1,0:T(1,128)}), f32[16,1,32]{2,1,0:T(1,128)S(1)}, u32[]{:S(2)}, u32[]{:S(2)}) %all-to-all-start.5) | async-done | bytes 2080 | tf_op jit(solution)/shard_map/all_to_all | solution.py:28
  54.3 3.5 %all-to-all-start.7 = ((f32[16,1,32]{2,1,0:T(1,128)}), f32[16,1,32]{2,1,0:T(1,128)S(1)}, u32[]{:S(2)}, u32[]{:S(2)}) async-start(f32[16,1,32]{2,1,0:T(1,128)} %bitcast.13), calls=%async_computation.7 | async-start | bytes 16384 | tf_op jit(solution)/shard_map/all_to_all | solution.py:28
  57.7 2.1 %reduce_sum.74 = f32[16,256,32]{1,2,0:T(8,128)} reduce(f32[2,16,256,32]{2,3,1,0:T(8,128)} %all_to_all.49, f32[]{:T(128)} %constant.6.clone.1), dimensions={0}, to_apply=%region_2.0 | reduce | flops 131072 | bytes 1572868 | tf_op jit(solution)/shard_map/reduce_sum | solution.py:22
  59.9 4.2 %all-to-all-done.7 = f32[16,1,32]{2,1,0:T(1,128)S(1)} async-done(((f32[16,1,32]{2,1,0:T(1,128)}), f32[16,1,32]{2,1,0:T(1,128)S(1)}, u32[]{:S(2)}, u32[]{:S(2)}) %all-to-all-start.7) | async-done | bytes 2080 | tf_op jit(solution)/shard_map/all_to_all | solution.py:28
  64.0 4.2 %all-to-all-start.3 = ((f32[16,256,32]{1,2,0:T(8,128)}), f32[16,256,32]{1,2,0:T(8,128)}, u32[]{:S(2)}, u32[]{:S(2)}) async-start(f32[16,256,32]{1,2,0:T(8,128)} %reduce_sum.74), calls=%async_computation.3 | async-start | bytes 1048576 | tf_op jit(solution)/shard_map/all_to_all | solution.py:28
  68.3 0.0 copy-start.6
  68.3 1.5 reduce_sum.72
  69.8 7.4 %all-to-all-done.3 = f32[16,256,32]{1,2,0:T(8,128)} async-done(((f32[16,256,32]{1,2,0:T(8,128)}), f32[16,256,32]{1,2,0:T(8,128)}, u32[]{:S(2)}, u32[]{:S(2)}) %all-to-all-start.3) | async-done | bytes 524320 | tf_op jit(solution)/shard_map/all_to_all | solution.py:28
  77.3 3.7 %all-to-all-start.1 = ((f32[16,32,768]{2,1,0:T(8,128)}), f32[16,32,768]{2,1,0:T(8,128)S(1)}, u32[]{:S(2)}, u32[]{:S(2)}) async-start(f32[16,32,768]{2,1,0:T(8,128)} %reduce_sum.72), calls=%async_computation.1 | async-start | bytes 3145728 | tf_op jit(solution)/shard_map/all_to_all | solution.py:28
  81.0 0.0 all-gather.2.cloned.1.call-start
  81.1 0.5 convert_bitcast_fusion.2
  81.6 0.1 copy.52
  81.7 0.5 convert_bitcast_fusion.1
  82.2 0.1 copy.53
  82.3 1.1 reduce_sum.75
  83.4 0.6 convert_bitcast_fusion
  84.1 16.0 %all-to-all-done.1 = f32[16,32,768]{2,1,0:T(8,128)S(1)} async-done(((f32[16,32,768]{2,1,0:T(8,128)}), f32[16,32,768]{2,1,0:T(8,128)S(1)}, u32[]{:S(2)}, u32[]{:S(2)}) %all-to-all-start.1) | async-done | bytes 1572896 | tf_op jit(solution)/shard_map/all_to_all | solution.py:28
  100.1 0.1 reduce_sum.73
  100.2 0.6 fusion.3
  100.9 0.7 concatenate.17
  101.6 0.0 all-gather.2.cloned.1.call-update
  101.6 46.9 %all-gather.2.cloned.1.call-done = bf16[1024,1026]{1,0:T(8,128)(2,1)} async-done(((bf16[32,1026]{1,0:T(8,128)(2,1)}), bf16[1024,1026]{1,0:T(8,128)(2,1)}) %all-gather.2.cloned.1.call-update) | async-done | bytes 2101264 | tf_op jit(solution)/shard_map/all_gather | solution.py:43
  148.5 2.7 %slice_bitcast_fusion = (bf16[256,1024]{0,1:T(8,128)(2,1)S(1)}, bf16[1024,256]{1,0:T(8,128)(2,1)}, bf16[1024,256]{1,0:T(8,128)(2,1)}, bf16[1024,256]{1,0:T(8,128)(2,1)}) fusion(bf16[1024,1026]{1,0:T(8,128)(2,1)} %all-gather.2.cloned.1.call-done), kind=kLoop, calls=%fused_computation.1 | loop fusion | bytes 4194304 | tf_op jit(solution)/shard_map/transpose | solution.py:46
  151.2 1.0 copy.54
  152.2 1.9 %slice_reduce_fusion = (bf16[1024]{0:T(1024)(128)(2,1)}, bf16[1024]{0:T(1024)(128)(2,1)}) fusion(bf16[1024,1026]{1,0:T(8,128)(2,1)} %all-gather.2.cloned.1.call-done), kind=kLoop, calls=%fused_computation.2 | loop fusion | bytes 8192 | tf_op jit(solution)/shard_map/slice | solution.py:45
  (19 shorter events, 0.1 us)
Async XLA Ops:
  9.8 8.8 %all-to-all-start.4 = ((f32[2,1,512]{2,1,0:T(1,128)}), f32[2,1,512]{2,1,0:T(1,128)S(1)}, u32[]{:S(2)}, u32[]{:S(2)}) async-start(f32[2,1,512]{2,1,0:T(1,128)} %reshape.72), calls=%async_computation.4 | async-start | bytes 8192 | tf_op jit(solution)/shard_map/all_to_all | solution.py:21
  18.6 5.4 %copy-start.4 = (f32[1,1024]{1,0:T(1,128)S(1)}, f32[1,1024]{1,0:T(1,128)}, u32[]{:S(2)}) copy-start(f32[1,1024]{1,0:T(1,128)} %param.17) | copy-start | bytes 12292
  18.6 11.7 %all-to-all-start = ((f32[2,16,32,768]{3,2,1,0:T(8,128)}), f32[2,16,32,768]{3,2,1,0:T(8,128)S(1)}, u32[]{:S(2)}, u32[]{:S(2)}) async-start(f32[2,16,32,768]{3,2,1,0:T(8,128)} %copy.46), calls=%async_computation | async-start | bytes 6291456 | tf_op jit(solution)/shard_map/all_to_all | solution.py:21
  40.2 14.1 %all-to-all-start.5 = ((f32[16,1,32]{2,1,0:T(1,128)}), f32[16,1,32]{2,1,0:T(1,128)S(1)}, u32[]{:S(2)}, u32[]{:S(2)}) async-start(f32[16,1,32]{2,1,0:T(1,128)} %bitcast.10), calls=%async_computation.5 | async-start | bytes 16384 | tf_op jit(solution)/shard_map/all_to_all | solution.py:28
  54.3 9.8 %all-to-all-start.7 = ((f32[16,1,32]{2,1,0:T(1,128)}), f32[16,1,32]{2,1,0:T(1,128)S(1)}, u32[]{:S(2)}, u32[]{:S(2)}) async-start(f32[16,1,32]{2,1,0:T(1,128)} %bitcast.13), calls=%async_computation.7 | async-start | bytes 16384 | tf_op jit(solution)/shard_map/all_to_all | solution.py:28
  64.0 13.2 %all-to-all-start.3 = ((f32[16,256,32]{1,2,0:T(8,128)}), f32[16,256,32]{1,2,0:T(8,128)}, u32[]{:S(2)}, u32[]{:S(2)}) async-start(f32[16,256,32]{1,2,0:T(8,128)} %reduce_sum.74), calls=%async_computation.3 | async-start | bytes 1048576 | tf_op jit(solution)/shard_map/all_to_all | solution.py:28
  68.3 12.8 %copy-start.5 = (f32[32]{0:T(128)S(1)}, f32[32]{0:T(128)}, u32[]{:S(2)}) copy-start(f32[32]{0:T(128)} %param.22) | copy-start | bytes 388
  68.3 13.4 %copy-start.6 = (f32[32]{0:T(128)S(1)}, f32[32]{0:T(128)}, u32[]{:S(2)}) copy-start(f32[32]{0:T(128)} %param.23) | copy-start | bytes 388
  68.3 15.1 %copy-start = (f32[256,32]{0,1:T(8,128)S(1)}, f32[256,32]{0,1:T(8,128)}, u32[]{:S(2)}) copy-start(f32[256,32]{0,1:T(8,128)} %param.21) | copy-start | bytes 98308
  69.8 30.4 %copy-start.1 = (f32[32,256]{1,0:T(8,128)S(1)}, f32[32,256]{1,0:T(8,128)}, u32[]{:S(2)}) copy-start(f32[32,256]{1,0:T(8,128)} %param.20) | copy-start | bytes 98308
  69.8 30.4 %copy-start.2 = (f32[32,256]{1,0:T(8,128)S(1)}, f32[32,256]{1,0:T(8,128)}, u32[]{:S(2)}) copy-start(f32[32,256]{1,0:T(8,128)} %param.19) | copy-start | bytes 98308
  69.8 30.4 %copy-start.3 = (f32[32,256]{1,0:T(8,128)S(1)}, f32[32,256]{1,0:T(8,128)}, u32[]{:S(2)}) copy-start(f32[32,256]{1,0:T(8,128)} %param.18) | copy-start | bytes 98308
  77.3 22.8 %all-to-all-start.1 = ((f32[16,32,768]{2,1,0:T(8,128)}), f32[16,32,768]{2,1,0:T(8,128)S(1)}, u32[]{:S(2)}, u32[]{:S(2)}) async-start(f32[16,32,768]{2,1,0:T(8,128)} %reduce_sum.72), calls=%async_computation.1 | async-start | bytes 3145728 | tf_op jit(solution)/shard_map/all_to_all | solution.py:28
  81.0 67.5 %all-gather.2.cloned.1.call-start = ((), (), s32[]{:S(2)}) async-start(), calls=%async_computation.8 | async-start | bytes 2433024 | tf_op jit(solution)/shard_map/all_gather | solution.py:43
Sparse Core Ops, SparseCore 0:
  101.7 46.7 all-gather.1
where the time goes:
time: 162 us; the launch traced here: 161 us
  waiting for transfers between devices  79.5 us (49%)
  starting transfers between devices  27.8 us (17%)
  local copies, waits for them, and re-layouts  15.6 us (10%)
  between operations  14.2 us (9%)
  other arithmetic  13.9 us (9%)
  blocking collectives  9.91 us (6%)
    all_gather x1, waiting for transfers between devices, gather_turned(): whole, at, done = (lax.all_gather(both, axis, axis=0, tiled=True), 0, [])  46.9 us
    all_to_all x4, waiting for transfers between devices, sum_by_axis(): return jnp.sum(lax.all_to_all(own, far, 0, 0, tiled=True), axis=0)  32.6 us
    all_to_all x4, starting transfers between devices, sum_by_axis(): return jnp.sum(lax.all_to_all(own, far, 0, 0, tiled=True), axis=0)  19.1 us
    all_to_all x2, blocking collectives, sent_and_summed(): tiles = lax.all_to_all(in_blocks(x, dim, count), axis, 0, 0, tiled=True)  9.91 us
    all_to_all x2, starting transfers between devices, sent_and_summed(): tiles = lax.all_to_all(in_blocks(x, dim, count), axis, 0, 0, tiled=True)  8.68 us
    unnamed x21, local copies, waits for them, and re-layouts  5 us
    reduce_sum x4, other arithmetic, sent_and_summed(): return jnp.sum(tiles, axis=0)  4.88 us
    transpose x4, local copies, waits for them, and re-layouts, in_blocks(): return jnp.moveaxis(tiles, dim, 0)  4.34 us
  transfers between devices with their start and end apart: 7, of which 5 were waited for; matrix products, arithmetic and copies ran while one was open for 12% of the time, Pallas kernels for 0%

commit v1 on v0

v1 whole, which is shorter than its diff:
```python
import math

import jax
import jax.numpy as jnp
from jax import lax
from jax.experimental import pallas as pl
from jax.experimental.pallas import tpu as pltpu
from jax.sharding import PartitionSpec as P

MESH = pl.DeviceIdType.MESH
F32 = jnp.float32
BF16 = jnp.bfloat16

RATE = 0.4 * 32**-0.5

SPREAD = 21.0
STEPS = 4096.0
SHIFT = 125.0
PAIR_TOP = 2.6
FOUR_TOP = 10.4


def encoded(x, top):
    log = jnp.log(1.0 + jnp.abs(x) * (STEPS / top))
    v = jnp.exp2(log * (SPREAD / math.log(2.0)) - SHIFT)
    return jnp.where(x < 0, -v, v).astype(BF16)


def decoded(code, top):
    v = code.astype(F32)
    log = jnp.log(jnp.abs(v))
    size = (jnp.exp2(log * (1.0 / (SPREAD * math.log(2.0))) + SHIFT / SPREAD) - 1.0) * (top / STEPS)
    return jnp.where(v < 0, -size, size)


def kernel(
    pm, pq, pk, pv, pn, pb, mm, mq, mk, mv, mn, mb,
    cm, cq, ck, cv, cn, cb, sm, sq, sk, sv, sn, sb,
    raw, flat, pair, send1, recv1, send2, recv2, acc, gat, mast,
    nbuf, npair, nx, nz, nmast,
    load_sem, mload_sem, nload_sem, d_send, d_recv,
    s1s, s1r, s2s, s2r, g1s, g1r, g2s, g2r, fs, fr, ns, nr,
):
    b = lax.axis_index("batch")
    col = lax.axis_index("cols")
    z, x, core = b // 8, (b // 2) % 4, b % 2

    def at(z, x, core):
        return (z * 8 + x * 2 + core, col)

    def step(h, j):
        return ((z, (x + j) % 4), (x + j) % 4) if h == 0 else (((z + j) % 4, x), (z + j) % 4)

    def wait(ref, sem):
        pltpu.make_async_copy(ref, ref, sem).wait()

    loads = [pltpu.make_async_copy(pm, flat, load_sem.at[0])]
    for a, ref in ((1, pq), (2, pk), (3, pv)):
        loads.append(pltpu.make_async_copy(ref, raw.at[a], load_sem.at[a]))
    small = [
        pltpu.make_async_copy(pn, nbuf.at[0], nload_sem.at[0]),
        pltpu.make_async_copy(pb, nbuf.at[1], nload_sem.at[1]),
        pltpu.make_async_copy(mn, nmast.at[0], nload_sem.at[2]),
        pltpu.make_async_copy(mb, nmast.at[1], nload_sem.at[3]),
    ]
    masters = [pltpu.make_async_copy(ref, mast.at[a], mload_sem.at[a]) for a, ref in enumerate((mm, mq, mk, mv))]
    loads[0].start()
    for copy in small:
        copy.start()
    for copy in loads[1:]:
        copy.start()
    for copy in masters:
        copy.start()

    barrier = pltpu.get_barrier_semaphore()
    peers = [at(z, x, 1 - core)]
    for j in (1, 2, 3):
        peers += [at(*step(0, j)[0], core), at(*step(1, j)[0], core)]
    for peer in peers:
        pl.semaphore_signal(barrier, inc=1, device_id=peer, device_id_type=MESH)

    for copy in small:
        copy.wait()
    lanes = lax.broadcasted_iota(jnp.int32, (8, 128), 1)
    rows = lax.broadcasted_iota(jnp.int32, (8, 128), 0)
    mine = (rows * 4 + lanes // 32) == b
    for i in range(2):
        m = jnp.concatenate([nmast[i]] * 4, axis=1)
        nbuf[i] = jnp.where(mine, jnp.broadcast_to(m, (8, 128)), 0.0) - RATE * nbuf[i]

    loads[0].wait()
    raw[0] = flat[...].T.reshape(16, 2, 32, 256)

    pl.semaphore_wait(barrier, 7)

    sends = []

    def remote(src, dst, ssem, rsem, dev):
        copy = pltpu.make_async_remote_copy(
            src_ref=src, dst_ref=dst, send_sem=ssem, recv_sem=rsem, device_id=dev, device_id_type=MESH
        )
        copy.start()
        sends.append(copy)

    partner = at(z, x, 1 - core)
    remote(nbuf, npair, ns.at[0], nr.at[0], partner)
    for a in range(4):
        if a:
            loads[a].wait()
        remote(raw.at[a, :, 1 - core], pair.at[a], d_send.at[a], d_recv.at[a], partner)

    def pair_sum(a, zi, xi, h):
        i = zi * 4 + xi
        c = slice(128 * h, 128 * h + 128)
        return raw[a, i, core, :, c] + pair[a, i, :, c]

    def block(a, h, first, second):
        return pair_sum(a, second, first, h) if h == 0 else pair_sum(a, first, second, h)

    def e1(a):
        wait(pair.at[a], d_recv.at[a])
        for h in range(2):
            here = x if h == 0 else z
            for j in (2, 1, 3):
                dev, to = step(h, j)
                for k in range(4):
                    send1[a, h, j - 1, k] = encoded(block(a, h, to, k), PAIR_TOP)
                remote(send1.at[a, h, j - 1], recv1.at[a, h, j - 1], s1s.at[a, h, j - 1], s1r.at[a, h], at(*dev, core))
            for k in range(4):
                acc[a, h, k] = block(a, h, here, k)

    def r1(a):
        for h in range(2):
            wait(recv1.at[a, h], s1r.at[a, h])
            own = z if h == 0 else x

            def total(k):
                t = acc[a, h, k]
                for j in range(3):
                    t += decoded(recv1[a, h, j, k], PAIR_TOP)
                return t

            for j in (2, 1, 3):
                dev, to = step(1 - h, j)
                send2[a, h, j - 1] = encoded(total(to), FOUR_TOP)
                remote(send2.at[a, h, j - 1], recv2.at[a, h, j - 1], s2s.at[a, h, j - 1], s2r.at[a, h], at(*dev, core))
            acc[a, h, 0] = total(own)

    stepped = (sm, sq, sk, sv)

    def r2(a):
        masters[a].wait()
        for h in range(2):
            wait(recv2.at[a, h], s2r.at[a, h])
            t = acc[a, h, 0]
            for j in range(3):
                t += decoded(recv2[a, h, j], FOUR_TOP)
            c = slice(128 * h, 128 * h + 128)
            new = mast[a, :, c] - RATE * t
            stepped[a][:, c] = new
            first, second = (x, z) if h == 0 else (z, x)
            own = gat.at[a, h, core, first, second]
            gat[a, h, core, first, second] = new.astype(BF16)
            for j in (2, 1, 3):
                dev, _ = step(1 - h, j)
                remote(own, own, g1s.at[a, h, j - 1], g1r.at[a, h], at(*dev, core))

    def g1(a):
        for h in range(2):
            first = x if h == 0 else z
            row = gat.at[a, h, core, first]
            wait(gat.at[a, h, core, 0, pl.ds(0, 3)], g1r.at[a, h])
            for j in (2, 1, 3):
                dev, _ = step(h, j)
                remote(row, row, g2s.at[a, h, j - 1], g2r.at[a, h, j - 1], at(*dev, core))
            remote(row, row, fs.at[a, h, 3], fr.at[a, h], partner)

    def g2(a):
        for h in range(2):
            for j in (1, 3, 2):
                first = ((x if h == 0 else z) - j + 4) % 4
                row = gat.at[a, h, core, first]
                wait(row, g2r.at[a, h, j - 1])
                remote(row, row, fs.at[a, h, j - 1], fr.at[a, h], partner)

    outs = (cm, cq, ck, cv)

    def f(a):
        for h in range(2):
            wait(gat.at[a, h, 0], fr.at[a, h])
        for h in range(2):
            c = slice(128 * h, 128 * h + 128)
            order = (1, 2, 0, 3, 4) if h == 0 else (0, 2, 1, 3, 4)
            if a:
                for zi in range(4):
                    for xi in range(4):
                        for k in range(2):
                            first, second = (xi, zi) if h == 0 else (zi, xi)
                            outs[a][zi, xi, k, :, c] = gat[a, h, k, first, second]
            else:
                for zi in range(4):
                    for xi in range(0, 4, 2):
                        parts = []
                        for xj in (xi, xi + 1):
                            for k in range(2):
                                first, second = (xj, zi) if h == 0 else (zi, xj)
                                parts.append(gat[a, h, k, first, second])
                        at_lane = (zi * 4 + xi) * 64
                        outs[a][c, at_lane : at_lane + 128] = jnp.concatenate(parts, axis=0).T

    def n1():
        wait(npair, nr.at[0])
        nx[x] = nbuf[...] + npair[...]
        for j in (2, 1, 3):
            dev, _ = step(0, j)
            remote(nx.at[x], nx.at[x], ns.at[j], nr.at[1], at(*dev, core))

    def n2():
        wait(nx.at[pl.ds(0, 3)], nr.at[1])
        nz[z] = ((nx[0] + nx[1]) + nx[2]) + nx[3]
        for j in (2, 1, 3):
            dev, _ = step(1, j)
            remote(nz.at[z], nz.at[z], ns.at[3 + j], nr.at[2], at(*dev, core))

    def n3():
        wait(nz.at[pl.ds(0, 3)], nr.at[2])
        new = ((nz[0] + nz[1]) + nz[2]) + nz[3]
        cn[...] = new[0].astype(BF16)
        cb[...] = new[1].astype(BF16)
        place = jnp.sum(jnp.where(mine[None], new, 0.0), axis=1)
        slot = ((place[:, 0:32] + place[:, 32:64]) + place[:, 64:96]) + place[:, 96:128]
        sn[...] = slot[0:1]
        sb[...] = slot[1:2]

    for t in range(9):
        if t == 1:
            n1()
        if t == 2:
            n2()
        if t == 3:
            n3()
        for stage, lag in ((e1, 0), (r1, 1), (r2, 2), (g1, 3), (g2, 4), (f, 5)):
            if 0 <= t - lag < 4:
                stage(t - lag)

    for copy in sends:
        copy.wait_send()


def per_device(pq, pk, pv, pm, pn, pb, mq, mk, mv, mm, mn, mb):
    blocks = (16, 2, 32, 256)
    hbm = pl.BlockSpec(memory_space=pl.ANY)
    vmem = pl.BlockSpec(memory_space=pltpu.VMEM)
    dma = pltpu.SemaphoreType.DMA
    gathered = jax.ShapeDtypeStruct((4, 4, 2, 32, 256), BF16)
    share = jax.ShapeDtypeStruct((32, 256), F32)
    small = jax.ShapeDtypeStruct((8, 128), BF16)
    slot = jax.ShapeDtypeStruct((1, 32), F32)
    out = pl.pallas_call(
        kernel,
        out_shape=(jax.ShapeDtypeStruct((256, 1024), BF16), gathered, gathered, gathered, small, small)
        + (share,) * 4
        + (slot,) * 2,
        in_specs=[hbm] * 12,
        out_specs=(vmem,) * 12,
        scratch_shapes=[
            pltpu.VMEM((4, *blocks), F32),
            pltpu.VMEM((256, 1024), F32),
            pltpu.VMEM((4, 16, 32, 256), F32),
            pltpu.VMEM((4, 2, 3, 4, 32, 128), BF16),
            pltpu.VMEM((4, 2, 3, 4, 32, 128), BF16),
            pltpu.VMEM((4, 2, 3, 32, 128), BF16),
            pltpu.VMEM((4, 2, 3, 32, 128), BF16),
            pltpu.VMEM((4, 2, 4, 32, 128), F32),
            pltpu.VMEM((4, 2, 2, 4, 4, 32, 128), BF16),
            pltpu.VMEM((4, 32, 256), F32),
            pltpu.VMEM((2, 8, 128), F32),
            pltpu.VMEM((2, 8, 128), F32),
            pltpu.VMEM((4, 2, 8, 128), F32),
            pltpu.VMEM((4, 2, 8, 128), F32),
            pltpu.VMEM((2, 1, 32), F32),
            dma((4,)),
            dma((4,)),
            dma((4,)),
            dma((4,)),
            dma((4,)),
            dma((4, 2, 3)),
            dma((4, 2)),
            dma((4, 2, 3)),
            dma((4, 2)),
            dma((4, 2, 3)),
            dma((4, 2)),
            dma((4, 2, 3)),
            dma((4, 2, 3)),
            dma((4, 2, 4)),
            dma((4, 2)),
            dma((7,)),
            dma((3,)),
        ],
        compiler_params=pltpu.CompilerParams(collective_id=0, has_side_effects=True, vmem_limit_bytes=60 * 2**20),
        name="step",
    )(
        pm[0], pq.reshape(blocks), pk.reshape(blocks), pv.reshape(blocks), pn.reshape(8, 128), pb.reshape(8, 128),
        mm.T, mq, mk, mv, mn.reshape(1, 32), mb.reshape(1, 32),
    )
    cm, cq, ck, cv, cn, cb, sm, sq, sk, sv, sn, sb = out
    whole = (1024, 256)
    return (
        cq.reshape(whole), ck.reshape(whole), cv.reshape(whole), cm, cn.reshape(1024), cb.reshape(1024),
        sq, sk, sv, sm.T, sn.reshape(32), sb.reshape(32),
    )


def solution(mesh):
    in_specs = (
        P("batch", None, "cols"),
        P("batch", None, "cols"),
        P("batch", None, "cols"),
        P("batch", "cols", None),
        P("batch", None),
        P("batch", None),
        P("batch", "cols"),
        P("batch", "cols"),
        P("batch", "cols"),
        P("cols", "batch"),
        P("batch"),
        P("batch"),
    )
    out_specs = (
        P(None, "cols"),
        P(None, "cols"),
        P(None, "cols"),
        P("cols", None),
        P(),
        P(),
        P("batch", "cols"),
        P("batch", "cols"),
        P("batch", "cols"),
        P("cols", "batch"),
        P("batch"),
        P("batch"),
    )
    return jax.shard_map(per_device, mesh=mesh, in_specs=in_specs, out_specs=out_specs, check_vma=False)
```

time: 162 us -> 48.7 us (0.30)
  waiting for transfers between devices: 79.5 us -> 0 us
  Pallas kernels: 0 us -> 36.9 us
  starting transfers between devices: 27.8 us -> 0 us
  other arithmetic: 13.9 us -> 0 us
  between operations: 14.2 us -> 0.68 us
  blocking collectives: 9.91 us -> 0 us
  local copies, waits for them, and re-layouts: 15.6 us -> 10.5 us
    all_gather x1 -> x0, waiting for transfers between devices: 46.9 us -> none  [gather_turned(): whole, at, done = (lax.all_gather(both, axis, axis=0, tiled=True), 0, [])]
    pallas_call x0 -> x1, Pallas kernels: none -> 36.9 us  [per_device(): pl.pallas_call(kernel, out_shape=(jax.ShapeDtypeStruct((256, 1024), BF16)...]
    all_to_all x6 -> x0, waiting for transfers between devices: 32.6 us -> none  [the longest x4 32.6 us: sum_by_axis(): return jnp.sum(lax.all_to_all(own, far, 0, 0, tiled=True), axis=0)]
    all_to_all x6 -> x0, starting transfers between devices: 27.8 us -> none  [the longest x4 19.1 us: sum_by_axis(): return jnp.sum(lax.all_to_all(own, far, 0, 0, tiled=True), axis=0)]
    all_to_all x2 -> x0, blocking collectives: 9.91 us -> none  [sent_and_summed(): tiles = lax.all_to_all(in_blocks(x, dim, count), axis, 0, 0, tiled=True)]
    transpose x5 -> x0, local copies, waits for them, and re-layouts: 7.05 us -> none  [the longest x4 4.34 us: in_blocks(): return jnp.moveaxis(tiles, dim, 0)]
    reduce_sum x8 -> x0, other arithmetic: 6.11 us -> none  [the longest x4 4.88 us: sent_and_summed(): return jnp.sum(tiles, axis=0)]
    unnamed x21 -> x34, local copies, waits for them, and re-layouts: 5 us -> 10.5 us
  transfers between devices with their start and end apart: 7 -> 0, of which waited for: 5 -> 0; matrix products, arithmetic and copies ran while one was open for 12% -> 0% of each run, Pallas kernels for 0% -> 0%
where the time goes in v1:
time: 48.7 us; the launch traced here: 48.2 us
  Pallas kernels  36.9 us (76%)
  local copies, waits for them, and re-layouts  10.5 us (22%)
  between operations  0.68 us (1%)
    pallas_call x1, Pallas kernels, per_device(): pl.pallas_call(kernel, out_shape=(jax.ShapeDtypeStruct((256, 1024), BF16)...  36.9 us
    unnamed x34, local copies, waits for them, and re-layouts  10.5 us

profile of v1, /device:TPU:1, one launch (start us, length us, event | category | flops | bytes accessed | tf_op | source)
XLA Modules:
  0.0 48.2 jit_solution(16633980395439599579)
XLA Ops:
  0.6 36.9 %step.1 = (bf16[256,1024]{1,0:T(8,128)(2,1)}, bf16[4,4,2,32,256]{4,3,2,1,0:T(8,128)(2,1)}, bf16[4,4,2,32,256]{4,3,2,1,0:T(8,128)(2,1)}, bf16[4,4,2,32,256]{4,3,2...) custom-call(f32[256,1024]{1,0:T(8,128)} %bitcast.17, ...), custom_call_target="tpu_custom_call" | custom-call | tf_op jit(solution)/shard_map/step/pallas_call | solution.py:259
  37.6 0.0 copy-start.2
  37.6 1.9 %copy.36 = bf16[1024,256]{1,0:T(8,128)(2,1)} copy(bf16[1024,256]{1,0:T(8,128)(2,1)} %bitcast.23) | data formatting | bytes 1048576
  39.5 0.0 copy-done.2
  39.5 0.0 copy-start.1
  39.5 0.8 %copy.37 = bf16[1024,256]{1,0:T(8,128)(2,1)} copy(bf16[1024,256]{1,0:T(8,128)(2,1)S(1)} %bitcast.22) | data formatting | bytes 1048576
  40.3 0.4 copy-done.1
  40.8 0.0 copy-start
  40.8 0.8 %copy.38 = bf16[1024,256]{1,0:T(8,128)(2,1)} copy(bf16[1024,256]{1,0:T(8,128)(2,1)S(1)} %bitcast.21) | data formatting | bytes 1048576
  41.6 0.4 copy-done
  42.0 0.0 copy-start.8
  42.0 0.0 copy-start.6
  42.0 0.8 %copy.39 = bf16[256,1024]{1,0:T(8,128)(2,1)} copy(bf16[256,1024]{1,0:T(8,128)(2,1)S(1)} %copy-done) | data formatting | bytes 1048576
  42.8 0.0 copy-done.8
  42.8 0.0 copy-start.7
  42.8 0.6 %copy.40 = bf16[1024]{0:T(1024)(128)(2,1)} copy(bf16[1024]{0:T(1024)(128)(2,1)S(1)} %bitcast.29) | data formatting | bytes 4096
  43.4 0.1 copy-done.7
  43.5 0.6 %copy.41 = bf16[1024]{0:T(1024)(128)(2,1)} copy(bf16[1024]{0:T(1024)(128)(2,1)S(1)} %bitcast.28) | data formatting | bytes 4096
  44.1 0.0 copy-done.6
  44.1 0.0 copy-start.5
  44.1 0.6 %copy.42 = f32[32,256]{1,0:T(8,128)} copy(f32[32,256]{1,0:T(8,128)S(1)} %copy-done.6) | data formatting | bytes 65536
  44.7 0.2 copy-done.5
  44.8 0.0 copy-start.4
  44.8 0.6 %copy.43 = f32[32,256]{1,0:T(8,128)} copy(f32[32,256]{1,0:T(8,128)S(1)} %copy-done.5) | data formatting | bytes 65536
  45.5 0.2 copy-done.4
  45.6 0.0 copy-start.3
  45.6 0.6 %copy.44 = f32[32,256]{1,0:T(8,128)} copy(f32[32,256]{1,0:T(8,128)S(1)} %copy-done.4) | data formatting | bytes 65536
  46.2 0.2 copy-done.3
  46.4 0.0 copy-start.10
  46.4 0.6 %copy.45 = f32[256,32]{0,1:T(8,128)} copy(f32[256,32]{0,1:T(8,128)S(1)} %bitcast.25) | data formatting | bytes 65536
  47.0 0.0 copy-done.10
  47.1 0.0 copy-start.9
  47.1 0.5 %copy.46 = f32[32]{0:T(128)} copy(f32[32]{0:T(128)S(1)} %bitcast.33) | data formatting | bytes 256
  47.6 0.1 copy-done.9
  47.7 0.5 %copy.47 = f32[32]{0:T(128)} copy(f32[32]{0:T(128)S(1)} %bitcast.32) | data formatting | bytes 256
Async XLA Ops:
  37.6 1.9 %copy-start.2 = (bf16[4,4,2,32,256]{4,3,2,1,0:T(8,128)(2,1)S(1)}, bf16[4,4,2,32,256]{4,3,2,1,0:T(8,128)(2,1)}, u32[]{:S(2)}) copy-start(bf16[4,4,2,32,256]{4,3,2,1,0:T(8,128)(2,1)} %get-tuple-element.25) | copy-start | bytes 1572868
  39.5 1.2 %copy-start.1 = (bf16[4,4,2,32,256]{4,3,2,1,0:T(8,128)(2,1)S(1)}, bf16[4,4,2,32,256]{4,3,2,1,0:T(8,128)(2,1)}, u32[]{:S(2)}) copy-start(bf16[4,4,2,32,256]{4,3,2,1,0:T(8,128)(2,1)} %get-tuple-element.26) | copy-start | bytes 1572868
  40.8 1.2 %copy-start = (bf16[256,1024]{1,0:T(8,128)(2,1)S(1)}, bf16[256,1024]{1,0:T(8,128)(2,1)}, u32[]{:S(2)}) copy-start(bf16[256,1024]{1,0:T(8,128)(2,1)} %get-tuple-element.51) | copy-start | bytes 1572868
  42.0 0.8 %copy-start.8 = (bf16[8,128]{1,0:T(8,128)(2,1)S(1)}, bf16[8,128]{1,0:T(8,128)(2,1)}, u32[]{:S(2)}) copy-start(bf16[8,128]{1,0:T(8,128)(2,1)} %get-tuple-element.28) | copy-start | bytes 6148
  42.0 2.1 %copy-start.6 = (f32[32,256]{1,0:T(8,128)S(1)}, f32[32,256]{1,0:T(8,128)}, u32[]{:S(2)}) copy-start(f32[32,256]{1,0:T(8,128)} %get-tuple-element.54) | copy-start | bytes 98308
  42.8 0.7 %copy-start.7 = (bf16[8,128]{1,0:T(8,128)(2,1)S(1)}, bf16[8,128]{1,0:T(8,128)(2,1)}, u32[]{:S(2)}) copy-start(bf16[8,128]{1,0:T(8,128)(2,1)} %get-tuple-element.29) | copy-start | bytes 6148
  44.1 0.8 %copy-start.5 = (f32[32,256]{1,0:T(8,128)S(1)}, f32[32,256]{1,0:T(8,128)}, u32[]{:S(2)}) copy-start(f32[32,256]{1,0:T(8,128)} %get-tuple-element.55) | copy-start | bytes 98308
  44.8 0.8 %copy-start.4 = (f32[32,256]{1,0:T(8,128)S(1)}, f32[32,256]{1,0:T(8,128)}, u32[]{:S(2)}) copy-start(f32[32,256]{1,0:T(8,128)} %get-tuple-element.56) | copy-start | bytes 98308
  45.6 0.8 %copy-start.3 = (f32[32,256]{1,0:T(8,128)S(1)}, f32[32,256]{1,0:T(8,128)}, u32[]{:S(2)}) copy-start(f32[32,256]{1,0:T(8,128)} %get-tuple-element.33) | copy-start | bytes 98308
  46.4 0.7 %copy-start.10 = (f32[1,32]{1,0:T(1,128)S(1)}, f32[1,32]{1,0:T(1,128)}, u32[]{:S(2)}) copy-start(f32[1,32]{1,0:T(1,128)} %get-tuple-element.34) | copy-start | bytes 388
  47.1 0.6 %copy-start.9 = (f32[1,32]{1,0:T(1,128)S(1)}, f32[1,32]{1,0:T(1,128)}, u32[]{:S(2)}) copy-start(f32[1,32]{1,0:T(1,128)} %get-tuple-element.35) | copy-start | bytes 388

commit v2 on v1

--- a/solution.py
+++ b/solution.py
@@ -247,6 +247,15 @@
         copy.wait_send()
 
 
+def placed(*refs):
+    sems = refs[24]
+    copies = [pltpu.make_async_copy(refs[i], refs[12 + i], sems.at[i]) for i in range(12)]
+    for copy in copies:
+        copy.start()
+    for copy in copies:
+        copy.wait()
+
+
 def per_device(pq, pk, pv, pm, pn, pb, mq, mk, mv, mm, mn, mb):
     blocks = (16, 2, 32, 256)
     hbm = pl.BlockSpec(memory_space=pl.ANY)
@@ -256,11 +265,11 @@
     share = jax.ShapeDtypeStruct((32, 256), F32)
     small = jax.ShapeDtypeStruct((8, 128), BF16)
     slot = jax.ShapeDtypeStruct((1, 32), F32)
+    shapes = (jax.ShapeDtypeStruct((256, 1024), BF16), gathered, gathered, gathered, small, small)
+    shapes += (share,) * 4 + (slot,) * 2
     out = pl.pallas_call(
         kernel,
-        out_shape=(jax.ShapeDtypeStruct((256, 1024), BF16), gathered, gathered, gathered, small, small)
-        + (share,) * 4
-        + (slot,) * 2,
+        out_shape=tuple(pltpu.VMEM(o.shape, o.dtype) for o in shapes),
         in_specs=[hbm] * 12,
         out_specs=(vmem,) * 12,
         scratch_shapes=[
@@ -303,7 +312,14 @@
         pm[0], pq.reshape(blocks), pk.reshape(blocks), pv.reshape(blocks), pn.reshape(8, 128), pb.reshape(8, 128),
         mm.T, mq, mk, mv, mn.reshape(1, 32), mb.reshape(1, 32),
     )
-    cm, cq, ck, cv, cn, cb, sm, sq, sk, sv, sn, sb = out
+    cm, cq, ck, cv, cn, cb, sm, sq, sk, sv, sn, sb = pl.pallas_call(
+        placed,
+        out_shape=shapes,
+        in_specs=[vmem] * 12,
+        out_specs=(hbm,) * 12,
+        scratch_shapes=[dma((12,))],
+        name="placed",
+    )(*[pltpu.with_memory_space_constraint(o, pltpu.VMEM) for o in out])
     whole = (1024, 256)
     return (
         cq.reshape(whole), ck.reshape(whole), cv.reshape(whole), cm, cn.reshape(1024), cb.reshape(1024),

time: 48.7 us -> 37.8 us (0.78)
  local copies, waits for them, and re-layouts: 10.5 us -> 0 us
    unnamed x34 -> x0, local copies, waits for them, and re-layouts: 10.5 us -> none
    pallas_call x1 -> x2, Pallas kernels: 36.9 us -> 37 us  [the longest x1 35.6 us: per_device(): pl.pallas_call(kernel, out_shape=tuple((pltpu.VMEM(o.shape, o.dtype) for...]
where the time goes in v2:
time: 37.8 us; the launch traced here: 37.7 us
  Pallas kernels  37 us (98%)
  between operations  0.66 us (2%)
    pallas_call x1, Pallas kernels, per_device(): pl.pallas_call(kernel, out_shape=tuple((pltpu.VMEM(o.shape, o.dtype) for...  35.6 us
    pallas_call x1, Pallas kernels, per_device(): pl.pallas_call(placed, out_shape=shapes, in_specs=[vmem] * 12, out_specs=...  1.47 us

profile of v2, /device:TPU:1, one launch (start us, length us, event | category | flops | bytes accessed | tf_op | source)
XLA Modules:
  0.0 37.7 jit_solution(1403712044229618179)
XLA Ops:
  0.6 35.6 %step.1 = (bf16[256,1024]{1,0:T(8,128)(2,1)S(1)}, bf16[4,4,2,32,256]{4,3,2,1,0:T(8,128)(2,1)S(1)}, bf16[4,4,2,32,256]{4,3,2,1,0:T(8,128)(2,1)S(1)}, bf16[4,4,2,3...) custom-call(f32[256,1024]{1,0:T(8,128)} %bitcast.17, ...), custom_call_target="tpu_custom_call" | custom-call | tf_op jit(solution)/shard_map/step/pallas_call | solution.py:270
  36.2 1.5 %placed.1 = (bf16[256,1024]{1,0:T(8,128)(2,1)}, bf16[4,4,2,32,256]{4,3,2,1,0:T(8,128)(2,1)}, bf16[4,4,2,32,256]{4,3,2,1,0:T(8,128)(2,1)}, bf16[4,4,2,32,256]{4,3...) custom-call(bf16[256,1024]{1,0:T(8,128)(2,1)S(1)} %get-tuple-element, ...), custom_call_target="tpu_custom_call" | custom-call | tf_op jit(solution)/shard_map/placed/pallas_call | solution.py:315

commit v3 on v2

v3 whole, which is shorter than its diff:
```python
import math

import jax
import jax.numpy as jnp
from jax import lax
from jax.experimental import pallas as pl
from jax.experimental.pallas import tpu as pltpu
from jax.sharding import PartitionSpec as P

MESH = pl.DeviceIdType.MESH
F32 = jnp.float32
BF16 = jnp.bfloat16

RATE = 0.4 * 32**-0.5

SPREAD = 21.0
STEPS = 4096.0
SHIFT = 125.0
PAIR_TOP = 2.6
ORDER = (2, 1, 3, 0)
BACK = (1, 3, 2)
FOUR_TOP = 10.4


def encoded(x, top):
    log = jnp.log(1.0 + jnp.abs(x) * (STEPS / top))
    v = jnp.exp2(log * (SPREAD / math.log(2.0)) - SHIFT)
    return jnp.where(x < 0, -v, v).astype(BF16)


def decoded(code, top):
    v = code.astype(F32)
    log = jnp.log(jnp.abs(v))
    size = (jnp.exp2(log * (1.0 / (SPREAD * math.log(2.0))) + SHIFT / SPREAD) - 1.0) * (top / STEPS)
    return jnp.where(v < 0, -size, size)


def kernel(
    pm, pq, pk, pv, pn, pb, mm, mq, mk, mv, mn, mb,
    cm, cq, ck, cv, cn, cb, sm, sq, sk, sv, sn, sb,
    raw, flat, pair, send1, recv1, send2, recv2, acc, gat, mast,
    nbuf, npair, nx, nz, nmast,
    load_sem, mload_sem, nload_sem, d_recv, s1r, s2r, g1r, g2r, fr, sent, ns, nr,
):
    b = lax.axis_index("batch")
    col = lax.axis_index("cols")
    z, x, core = b // 8, (b // 2) % 4, b % 2
    first, second = (x, z), (z, x)

    def at(z, x, core):
        return (z * 8 + x * 2 + core, col)

    def ahead(axis, j):
        return at(z, (x + j) % 4, core) if axis == 0 else at((z + j) % 4, x, core)

    def wait(ref, sem):
        pltpu.make_async_copy(ref, ref, sem).wait()

    def remote(src, dst, ssem, rsem, dev):
        pltpu.make_async_remote_copy(
            src_ref=src, dst_ref=dst, send_sem=ssem, recv_sem=rsem, device_id=dev, device_id_type=MESH
        ).start()

    def lanes_of(h):
        return slice(128 * h, 128 * h + 128)

    barrier = pltpu.get_barrier_semaphore()
    partner = at(z, x, 1 - core)
    for peer in [partner] + [ahead(axis, j) for j in (2, 1, 3) for axis in (0, 1)]:
        pl.semaphore_signal(barrier, inc=1, device_id=peer, device_id_type=MESH)

    turned = pltpu.make_async_copy(pm, flat, load_sem.at[0])
    loads = {a: pltpu.make_async_copy(ref, raw.at[a], load_sem.at[a]) for a, ref in ((1, pq), (2, pk), (3, pv))}
    small = [
        pltpu.make_async_copy(pn, nbuf.at[0], nload_sem.at[0]),
        pltpu.make_async_copy(pb, nbuf.at[1], nload_sem.at[1]),
        pltpu.make_async_copy(mn, nmast.at[0], nload_sem.at[2]),
        pltpu.make_async_copy(mb, nmast.at[1], nload_sem.at[3]),
    ]
    masters = [pltpu.make_async_copy(ref, mast.at[a], mload_sem.at[a]) for a, ref in enumerate((mm, mq, mk, mv))]
    for copy in (turned, *small, loads[1], loads[2], loads[3], *masters):
        copy.start()

    for copy in small:
        copy.wait()
    lanes = lax.broadcasted_iota(jnp.int32, (8, 128), 1)
    rows = lax.broadcasted_iota(jnp.int32, (8, 128), 0)
    mine = (rows * 4 + lanes // 32) == b
    for i in range(2):
        m = jnp.concatenate([nmast[i]] * 4, axis=1)
        nbuf[i] = jnp.where(mine, jnp.broadcast_to(m, (8, 128)), 0.0) - RATE * nbuf[i]

    def piece(a_ref, h, k, core):
        return a_ref.at[:, k, :, core, :, lanes_of(h)] if h == 0 else a_ref.at[:, :, k, core, :, lanes_of(h)]

    turned.wait()
    raw[0] = flat[...].T.reshape(4, 4, 2, 32, 256)
    for a in (1, 2, 3):
        loads[a].wait()
    pl.semaphore_wait(barrier, 7)
    for r in ORDER:
        for h in range(2):
            k = (second[h] + r) % 4
            remote(piece(raw, h, k, 1 - core), pair.at[h, k], sent.at[0], d_recv.at[h, r], partner)
        if r == 1:
            remote(nbuf, npair, ns.at[0], nr.at[0], partner)

    def block(a, h, f, k):
        zi, xi = (k, f) if h == 0 else (f, k)
        return raw[a, zi, xi, core, :, lanes_of(h)] + pair[h, k, a, f]

    def e1(h, r):
        k = (second[h] + r) % 4
        wait(pair.at[h, k], d_recv.at[h, r])
        for j in (2, 1, 3):
            for a in range(4):
                send1[h, r, j - 1, a] = encoded(block(a, h, (first[h] + j) % 4, k), PAIR_TOP)
            remote(send1.at[h, r, j - 1], recv1.at[h, r, j - 1], sent.at[1], s1r.at[h, r], ahead(h, j))

    def r1(h, r):
        k = (second[h] + r) % 4
        wait(recv1.at[h, r], s1r.at[h, r])
        for a in range(4):
            t = block(a, h, first[h], k)
            for j in range(3):
                t += decoded(recv1[h, r, j, a], PAIR_TOP)
            if r:
                send2[h, r - 1, a] = encoded(t, FOUR_TOP)
            else:
                acc[h, a] = t
        if r:
            remote(send2.at[h, r - 1], recv2.at[h, r - 1], sent.at[2], s2r.at[h], ahead(1 - h, r))

    stepped = (sm, sq, sk, sv)

    def r2(h):
        wait(recv2.at[h], s2r.at[h])
        for a in range(4):
            t = acc[h, a]
            for j in range(3):
                t += decoded(recv2[h, j, a], FOUR_TOP)
            new = mast[a, :, lanes_of(h)] - RATE * t
            stepped[a][:, lanes_of(h)] = new
            gat[h, core, first[h], second[h], a] = new.astype(BF16)
        part = gat.at[h, core, first[h], second[h]]
        for j in (2, 1, 3):
            remote(part, part, sent.at[3], g1r.at[h, j - 1], ahead(1 - h, j))

    def back(axis, h, j):
        return ((first, second)[axis][h] + 4 - j) % 4

    def spread(h, r):
        part = gat.at[h, core, first[h], back(1, h, r)]
        for j in (2, 1, 3):
            remote(part, part, sent.at[4], g2r.at[h, j - 1, r], ahead(h, j))

    def hand_over(h, j, r):
        part = gat.at[h, core, back(0, h, j), back(1, h, r)]
        remote(part, part, sent.at[5], fr.at[h, j, r], partner)

    outs = (cm, cq, ck, cv)

    def place(h, k, j, r):
        f, s = back(0, h, j), back(1, h, r)
        zi, xi = (s, f) if h == 0 else (f, s)
        for a in (1, 2, 3):
            outs[a][zi, xi, k, :, lanes_of(h)] = gat[h, k, f, s, a]

    def g1(h, r):
        wait(gat.at[h, core, first[h], back(1, h, r)], g1r.at[h, r - 1])
        spread(h, r)
        hand_over(h, 0, r)
        place(h, core, 0, r)

    def g2(h, j, r):
        wait(gat.at[h, core, back(0, h, j), back(1, h, r)], g2r.at[h, j - 1, r])
        hand_over(h, j, r)
        place(h, core, j, r)

    def last(h, j, r):
        wait(gat.at[h, 1 - core, back(0, h, j), back(1, h, r)], fr.at[h, j, r])
        place(h, 1 - core, j, r)

    def turn_back(h, zi, xi):
        parts = []
        for xj in (xi, xi + 1):
            for k in range(2):
                f, s = (xj, zi) if h == 0 else (zi, xj)
                parts.append(gat[h, k, f, s, 0])
        lane = (zi * 4 + xi) * 64
        cm[lanes_of(h), lane : lane + 128] = jnp.concatenate(parts, axis=0).T

    def n1():
        wait(npair, nr.at[0])
        nx[x] = nbuf[...] + npair[...]
        for j in (2, 1, 3):
            remote(nx.at[x], nx.at[x], ns.at[1], nr.at[1], ahead(0, j))

    def n2():
        wait(nx.at[pl.ds(0, 3)], nr.at[1])
        nz[z] = ((nx[0] + nx[1]) + nx[2]) + nx[3]
        for j in (2, 1, 3):
            remote(nz.at[z], nz.at[z], ns.at[2], nr.at[2], ahead(1, j))

    def n3():
        wait(nz.at[pl.ds(0, 3)], nr.at[2])
        new = ((nz[0] + nz[1]) + nz[2]) + nz[3]
        cn[...] = new[0].astype(BF16)
        cb[...] = new[1].astype(BF16)
        place = jnp.sum(jnp.where(mine[None], new, 0.0), axis=1)
        slot = ((place[:, 0:32] + place[:, 32:64]) + place[:, 64:96]) + place[:, 96:128]
        sn[...] = slot[0:1]
        sb[...] = slot[1:2]

    for r in ORDER:
        for h in range(2):
            e1(h, r)
    n1()
    for r in ORDER:
        for h in range(2):
            r1(h, r)
    n2()
    for copy in masters:
        copy.wait()
    for h in range(2):
        r2(h)
    for h in range(2):
        spread(h, 0)
        hand_over(h, 0, 0)
        place(h, core, 0, 0)
    n3()
    for r in BACK:
        for h in range(2):
            g1(h, r)
    for r in (0, *BACK):
        for j in BACK:
            for h in range(2):
                g2(h, j, r)
    for i, ref in enumerate((pair, send1, send2, send2, send1)):
        wait(ref, sent.at[i])
    wait(nbuf, ns.at[0])
    wait(nx.at[pl.ds(0, 3)], ns.at[1])
    wait(nz.at[pl.ds(0, 3)], ns.at[2])
    for r in (0, *BACK):
        for j in (0, *BACK):
            for h in range(2):
                last(h, j, r)
    for h in range(2):
        for zi in range(4):
            for xi in (0, 2):
                turn_back(h, zi, xi)
    wait(gat.at[0], sent.at[5])


def placed(*refs):
    sems = refs[24]
    copies = [pltpu.make_async_copy(refs[i], refs[12 + i], sems.at[i]) for i in range(12)]
    for copy in copies:
        copy.start()
    for copy in copies:
        copy.wait()


def per_device(pq, pk, pv, pm, pn, pb, mq, mk, mv, mm, mn, mb):
    blocks = (4, 4, 2, 32, 256)
    hbm = pl.BlockSpec(memory_space=pl.ANY)
    vmem = pl.BlockSpec(memory_space=pltpu.VMEM)
    dma = pltpu.SemaphoreType.DMA
    gathered = jax.ShapeDtypeStruct((4, 4, 2, 32, 256), BF16)
    share = jax.ShapeDtypeStruct((32, 256), F32)
    small = jax.ShapeDtypeStruct((8, 128), BF16)
    slot = jax.ShapeDtypeStruct((1, 32), F32)
    shapes = (jax.ShapeDtypeStruct((256, 1024), BF16), gathered, gathered, gathered, small, small)
    shapes += (share,) * 4 + (slot,) * 2
    out = pl.pallas_call(
        kernel,
        out_shape=tuple(pltpu.VMEM(o.shape, o.dtype) for o in shapes),
        in_specs=[hbm] * 12,
        out_specs=(vmem,) * 12,
        scratch_shapes=[
            pltpu.VMEM((4, *blocks), F32),
            pltpu.VMEM((256, 1024), F32),
            pltpu.VMEM((2, 4, 4, 4, 32, 128), F32),
            pltpu.VMEM((2, 4, 3, 4, 32, 128), BF16),
            pltpu.VMEM((2, 4, 3, 4, 32, 128), BF16),
            pltpu.VMEM((2, 3, 4, 32, 128), BF16),
            pltpu.VMEM((2, 3, 4, 32, 128), BF16),
            pltpu.VMEM((2, 4, 32, 128), F32),
            pltpu.VMEM((2, 2, 4, 4, 4, 32, 128), BF16),
            pltpu.VMEM((4, 32, 256), F32),
            pltpu.VMEM((2, 8, 128), F32),
            pltpu.VMEM((2, 8, 128), F32),
            pltpu.VMEM((4, 2, 8, 128), F32),
            pltpu.VMEM((4, 2, 8, 128), F32),
            pltpu.VMEM((2, 1, 32), F32),
            dma((4,)),
            dma((4,)),
            dma((4,)),
            dma((2, 4)),
            dma((2, 4)),
            dma((2,)),
            dma((2, 3)),
            dma((2, 3, 4)),
            dma((2, 4, 4)),
            dma((6,)),
            dma((3,)),
            dma((3,)),
        ],
        compiler_params=pltpu.CompilerParams(collective_id=0, has_side_effects=True, vmem_limit_bytes=60 * 2**20),
        name="step",
    )(
        pm[0], pq.reshape(blocks), pk.reshape(blocks), pv.reshape(blocks), pn.reshape(8, 128), pb.reshape(8, 128),
        mm.T, mq, mk, mv, mn.reshape(1, 32), mb.reshape(1, 32),
    )
    cm, cq, ck, cv, cn, cb, sm, sq, sk, sv, sn, sb = pl.pallas_call(
        placed,
        out_shape=shapes,
        in_specs=[vmem] * 12,
        out_specs=(hbm,) * 12,
        scratch_shapes=[dma((12,))],
        name="placed",
    )(*[pltpu.with_memory_space_constraint(o, pltpu.VMEM) for o in out])
    whole = (1024, 256)
    return (
        cq.reshape(whole), ck.reshape(whole), cv.reshape(whole), cm, cn.reshape(1024), cb.reshape(1024),
        sq, sk, sv, sm.T, sn.reshape(32), sb.reshape(32),
    )


def solution(mesh):
    in_specs = (
        P("batch", None, "cols"),
        P("batch", None, "cols"),
        P("batch", None, "cols"),
        P("batch", "cols", None),
        P("batch", None),
        P("batch", None),
        P("batch", "cols"),
        P("batch", "cols"),
        P("batch", "cols"),
        P("cols", "batch"),
        P("batch"),
        P("batch"),
    )
    out_specs = (
        P(None, "cols"),
        P(None, "cols"),
        P(None, "cols"),
        P("cols", None),
        P(),
        P(),
        P("batch", "cols"),
        P("batch", "cols"),
        P("batch", "cols"),
        P("cols", "batch"),
        P("batch"),
        P("batch"),
    )
    return jax.shard_map(per_device, mesh=mesh, in_specs=in_specs, out_specs=out_specs, check_vma=False)
```

time: 37.8 us -> 33.6 us (0.89)
  Pallas kernels: 37 us -> 32.9 us
    pallas_call x1, Pallas kernels: 35.6 us -> 31.4 us  [per_device(): pl.pallas_call(kernel, out_shape=tuple((pltpu.VMEM(o.shape, o.dtype) for...]
where the time goes in v3:
time: 33.6 us; the launch traced here: 33.5 us
  Pallas kernels  32.9 us (98%)
  between operations  0.66 us (2%)
    pallas_call x1, Pallas kernels, per_device(): pl.pallas_call(kernel, out_shape=tuple((pltpu.VMEM(o.shape, o.dtype) for...  31.4 us
    pallas_call x1, Pallas kernels, per_device(): pl.pallas_call(placed, out_shape=shapes, in_specs=[vmem] * 12, out_specs=...  1.47 us

profile of v3, /device:TPU:1, one launch (start us, length us, event | category | flops | bytes accessed | tf_op | source)
XLA Modules:
  0.0 33.5 jit_solution(4608473616614625020)
XLA Ops:
  0.6 31.4 %step.1 = (bf16[256,1024]{1,0:T(8,128)(2,1)S(1)}, bf16[4,4,2,32,256]{4,3,2,1,0:T(8,128)(2,1)S(1)}, bf16[4,4,2,32,256]{4,3,2,1,0:T(8,128)(2,1)S(1)}, bf16[4,4,2,3...) custom-call(f32[256,1024]{1,0:T(8,128)} %bitcast.17, ...), custom_call_target="tpu_custom_call" | custom-call | tf_op jit(solution)/shard_map/step/pallas_call | solution.py:275
  32.1 1.5 %placed.1 = (bf16[256,1024]{1,0:T(8,128)(2,1)}, bf16[4,4,2,32,256]{4,3,2,1,0:T(8,128)(2,1)}, bf16[4,4,2,32,256]{4,3,2,1,0:T(8,128)(2,1)}, bf16[4,4,2,32,256]{4,3...) custom-call(bf16[256,1024]{1,0:T(8,128)(2,1)S(1)} %get-tuple-element, ...), custom_call_target="tpu_custom_call" | custom-call | tf_op jit(solution)/shard_map/placed/pallas_call | solution.py:315

commit v4 on v3

v4 whole, which is shorter than its diff:
```python
import math

import jax
import jax.numpy as jnp
from jax import lax
from jax.experimental import pallas as pl
from jax.experimental.pallas import tpu as pltpu
from jax.sharding import PartitionSpec as P

MESH = pl.DeviceIdType.MESH
F32 = jnp.float32
BF16 = jnp.bfloat16

RATE = 0.4 * 32**-0.5

SPREAD = 21.0
STEPS = 4096.0
SHIFT = 125.0
PAIR_TOP = 2.6
ORDER = (2, 1, 3, 0)
BACK = (1, 3, 2)
FOUR_TOP = 10.4


def encoded(x, top):
    log = jnp.log(1.0 + jnp.abs(x) * (STEPS / top))
    v = jnp.exp2(log * (SPREAD / math.log(2.0)) - SHIFT)
    return jnp.where(x < 0, -v, v).astype(BF16)


def decoded(code, top):
    v = code.astype(F32)
    log = jnp.log(jnp.abs(v))
    size = (jnp.exp2(log * (1.0 / (SPREAD * math.log(2.0))) + SHIFT / SPREAD) - 1.0) * (top / STEPS)
    return jnp.where(v < 0, -size, size)


def kernel(
    pm, pq, pk, pv, pn, pb, mm, mq, mk, mv, mn, mb,
    cm, cq, ck, cv, cn, cb, sm, sq, sk, sv, sn, sb,
    raw, flat, pair, send1, recv1, send2, recv2, acc, gat, mast,
    nbuf, npair, nx, nz, nmast,
    load_sem, mload_sem, nload_sem, d_recv, s1r, s2r, g1r, g2r, fr, sent, ns, nr, hands,
):
    b = lax.axis_index("batch")
    col = lax.axis_index("cols")
    z, x, core = b // 8, (b // 2) % 4, b % 2
    first, second = (x, z), (z, x)

    def at(z, x, core):
        return (z * 8 + x * 2 + core, col)

    def ahead(axis, j):
        return at(z, (x + j) % 4, core) if axis == 0 else at((z + j) % 4, x, core)

    def wait(ref, sem):
        pltpu.make_async_copy(ref, ref, sem).wait()

    def remote(src, dst, ssem, rsem, dev):
        pltpu.make_async_remote_copy(
            src_ref=src, dst_ref=dst, send_sem=ssem, recv_sem=rsem, device_id=dev, device_id_type=MESH
        ).start()

    def lanes_of(h):
        return slice(128 * h, 128 * h + 128)

    def piece(ref, h, k, core=None):
        cores = slice(None) if core is None else core
        return ref.at[k, :, cores, :, lanes_of(h)] if h == 0 else ref.at[:, k, cores, :, lanes_of(h)]

    def pieces(g, h, k, core):
        ref = raw.at[g]
        return ref.at[:, k, :, core, :, lanes_of(h)] if h == 0 else ref.at[:, :, k, core, :, lanes_of(h)]

    barrier = pltpu.get_barrier_semaphore()
    partner = at(z, x, 1 - core)
    far = [ahead(axis, j) for j in (2, 1, 3) for axis in (0, 1)]

    @pl.when(core == 1)
    def _():
        pl.semaphore_signal(barrier, inc=1, device_id=partner, device_id_type=MESH)

    turned = pltpu.make_async_copy(pm, flat, mload_sem.at[4])
    loads = {
        (h, r, i): pltpu.make_async_copy(
            piece(ref, h, (second[h] + r) % 4), piece(raw.at[0, i], h, (second[h] + r) % 4), load_sem.at[h, r, i]
        )
        for r in ORDER
        for h in range(2)
        for i, ref in enumerate((pq, pk))
    }
    value = pltpu.make_async_copy(pv, raw.at[1, 1], mload_sem.at[5])
    small = [
        pltpu.make_async_copy(pn, nbuf.at[0], nload_sem.at[0]),
        pltpu.make_async_copy(pb, nbuf.at[1], nload_sem.at[1]),
        pltpu.make_async_copy(mn, nmast.at[0], nload_sem.at[2]),
        pltpu.make_async_copy(mb, nmast.at[1], nload_sem.at[3]),
    ]
    masters = [pltpu.make_async_copy(ref, mast.at[a], mload_sem.at[a]) for a, ref in enumerate((mq, mk, mm, mv))]
    for copy in (*loads.values(), *small, turned, value, *masters):
        copy.start()

    def share(g, h, r):
        k = (second[h] + r) % 4
        remote(pieces(g, h, k, 1 - core), pair.at[g, h, k], sent.at[0], d_recv.at[g, h, r], partner)

    @pl.when(core == 0)
    def _():
        pl.semaphore_wait(barrier, 1)
        pl.semaphore_signal(hands, inc=1, device_id=partner, device_id_type=MESH)

    @pl.when(core == 1)
    def _():
        pl.semaphore_wait(hands, 1)
        for peer in far:
            pl.semaphore_signal(barrier, inc=1, device_id=peer, device_id_type=MESH)

    for r in ORDER:
        for h in range(2):
            for i in range(2):
                loads[h, r, i].wait()
            share(0, h, r)

    for copy in small:
        copy.wait()
    lanes = lax.broadcasted_iota(jnp.int32, (8, 128), 1)
    rows = lax.broadcasted_iota(jnp.int32, (8, 128), 0)
    mine = (rows * 4 + lanes // 32) == b
    for i in range(2):
        m = jnp.concatenate([nmast[i]] * 4, axis=1)
        nbuf[i] = jnp.where(mine, jnp.broadcast_to(m, (8, 128)), 0.0) - RATE * nbuf[i]
    remote(nbuf, npair, ns.at[0], nr.at[0], partner)

    def turn(c):
        raw[1, 0, c] = flat[:, 256 * c : 256 * c + 256].T.reshape(4, 2, 32, 256)

    def block(g, i, h, f, k):
        zi, xi = (k, f) if h == 0 else (f, k)
        return raw[g, i, zi, xi, core, :, lanes_of(h)] + pair[g, h, k, i, f]

    def e1(g, h, r):
        k = (second[h] + r) % 4
        wait(pair.at[g, h, k], d_recv.at[g, h, r])
        for j in (2, 1, 3):
            for i in range(2):
                send1[g, h, r, j - 1, i] = encoded(block(g, i, h, (first[h] + j) % 4, k), PAIR_TOP)
            remote(send1.at[g, h, r, j - 1], recv1.at[g, h, r, j - 1], sent.at[1], s1r.at[g, h, r], ahead(h, j))

    def r1(g, h, r):
        k = (second[h] + r) % 4
        wait(recv1.at[g, h, r], s1r.at[g, h, r])
        for i in range(2):
            t = block(g, i, h, first[h], k)
            for j in range(3):
                t += decoded(recv1[g, h, r, j, i], PAIR_TOP)
            if r:
                send2[g, h, r - 1, i] = encoded(t, FOUR_TOP)
            else:
                acc[g, h, i] = t
        if r:
            remote(send2.at[g, h, r - 1], recv2.at[g, h, r - 1], sent.at[2], s2r.at[g, h], ahead(1 - h, r))

    stepped = (sq, sk, sm, sv)

    def r2(g, h):
        wait(recv2.at[g, h], s2r.at[g, h])
        for i in range(2):
            t = acc[g, h, i]
            for j in range(3):
                t += decoded(recv2[g, h, j, i], FOUR_TOP)
            new = mast[2 * g + i, :, lanes_of(h)] - RATE * t
            stepped[2 * g + i][:, lanes_of(h)] = new
            gat[g, h, core, first[h], second[h], i] = new.astype(BF16)
        part = gat.at[g, h, core, first[h], second[h]]
        for j in (2, 1, 3):
            remote(part, part, sent.at[3], g1r.at[g, h, j - 1], ahead(1 - h, j))

    def back(axis, h, j):
        return ((first, second)[axis][h] + 4 - j) % 4

    def spread(g, h, r):
        part = gat.at[g, h, core, first[h], back(1, h, r)]
        for j in (2, 1, 3):
            remote(part, part, sent.at[4], g2r.at[g, h, j - 1, r], ahead(h, j))

    def hand_over(g, h, j, r):
        part = gat.at[g, h, core, back(0, h, j), back(1, h, r)]
        remote(part, part, sent.at[5], fr.at[g, h, j, r], partner)

    outs = (cq, ck, cm, cv)

    def place(g, h, k, j, r):
        f, s = back(0, h, j), back(1, h, r)
        zi, xi = (s, f) if h == 0 else (f, s)
        for i in range(2):
            if 2 * g + i != 2:
                outs[2 * g + i][zi, xi, k, :, lanes_of(h)] = gat[g, h, k, f, s, i]

    def own(g, h):
        spread(g, h, 0)
        hand_over(g, h, 0, 0)
        place(g, h, core, 0, 0)

    def g1(g, h, r):
        wait(gat.at[g, h, core, first[h], back(1, h, r)], g1r.at[g, h, r - 1])
        spread(g, h, r)
        hand_over(g, h, 0, r)
        place(g, h, core, 0, r)

    def g2(g, h, j, r):
        wait(gat.at[g, h, core, back(0, h, j), back(1, h, r)], g2r.at[g, h, j - 1, r])
        hand_over(g, h, j, r)
        place(g, h, core, j, r)

    def last(g, h, j, r):
        wait(gat.at[g, h, 1 - core, back(0, h, j), back(1, h, r)], fr.at[g, h, j, r])
        place(g, h, 1 - core, j, r)

    def turn_back(h, zi, xi):
        parts = []
        for xj in (xi, xi + 1):
            for k in range(2):
                f, s = (xj, zi) if h == 0 else (zi, xj)
                parts.append(gat[1, h, k, f, s, 0])
        lane = pl.multiple_of((zi * 4 + xi) * 64, 128)
        cm[lanes_of(h), pl.ds(lane, 128)] = jnp.concatenate(parts, axis=0).T

    def finish(g, r):
        for j in (0, *BACK):
            for h in range(2):
                last(g, h, j, r)
        if g == 1:
            for xi in (0, 2):
                turn_back(0, back(1, 0, r), xi)

    def n1():
        wait(npair, nr.at[0])
        nx[x] = nbuf[...] + npair[...]
        for j in (2, 1, 3):
            remote(nx.at[x], nx.at[x], ns.at[1], nr.at[1], ahead(0, j))

    def n2():
        wait(nx.at[pl.ds(0, 3)], nr.at[1])
        nz[z] = ((nx[0] + nx[1]) + nx[2]) + nx[3]
        for j in (2, 1, 3):
            remote(nz.at[z], nz.at[z], ns.at[2], nr.at[2], ahead(1, j))

    def n3():
        wait(nz.at[pl.ds(0, 3)], nr.at[2])
        new = ((nz[0] + nz[1]) + nz[2]) + nz[3]
        cn[...] = new[0].astype(BF16)
        cb[...] = new[1].astype(BF16)
        place = jnp.sum(jnp.where(mine[None], new, 0.0), axis=1)
        slot = ((place[:, 0:32] + place[:, 32:64]) + place[:, 64:96]) + place[:, 96:128]
        sn[...] = slot[0:1]
        sb[...] = slot[1:2]

    both = range(2)

    def over(stage, g, *choices):
        for c in choices:
            for h in both:
                stage(g, h, *(c if isinstance(c, tuple) else (c,)))

    def gathered(g):
        before = None
        for r in (0, *BACK):
            over(g2, g, *((j, r) for j in BACK))
            if before is not None:
                finish(g, before)
            before = r

    @pl.when(core == 1)
    def _():
        pl.semaphore_wait(barrier, 6)
        pl.semaphore_signal(hands, inc=1, device_id=partner, device_id_type=MESH)

    @pl.when(core == 0)
    def _():
        pl.semaphore_wait(hands, 1)

    over(e1, 0, 2)
    turned.wait()
    turn(0)
    turn(1)
    over(e1, 0, 1)
    turn(2)
    turn(3)
    value.wait()
    over(share, 1, *ORDER)
    over(e1, 0, 3, 0)
    over(e1, 1, *ORDER)
    n1()
    over(r1, 0, *ORDER)
    for copy in masters:
        copy.wait()
    over(r1, 1, *ORDER)
    over(r2, 0, ())
    over(own, 0, ())
    n2()
    over(r2, 1, ())
    over(own, 1, ())
    over(g1, 0, 1, 3, 2)
    over(g1, 1, 1, 3, 2)
    n3()
    gathered(0)
    over(g2, 1, *((j, 0) for j in BACK))
    over(g2, 1, *((j, 1) for j in BACK))
    finish(1, 0)
    finish(0, 2)
    over(g2, 1, *((j, 3) for j in BACK))
    finish(1, 1)
    over(g2, 1, *((j, 2) for j in BACK))
    finish(1, 3)
    for zi in range(4):
        turn_back(1, zi, x // 2 * 2)
    for i, ref in enumerate((pair, send1, send2, send2, send1)):
        wait(ref, sent.at[i])
    wait(nbuf, ns.at[0])
    wait(nx.at[pl.ds(0, 3)], ns.at[1])
    wait(nz.at[pl.ds(0, 3)], ns.at[2])
    finish(1, 2)
    for zi in range(4):
        turn_back(1, zi, 2 - x // 2 * 2)
    wait(gat.at[:, 0], sent.at[5])


def placed(*refs):
    sems = refs[24]
    copies = [pltpu.make_async_copy(refs[i], refs[12 + i], sems.at[i]) for i in range(12)]
    for copy in copies:
        copy.start()
    for copy in copies:
        copy.wait()


def per_device(pq, pk, pv, pm, pn, pb, mq, mk, mv, mm, mn, mb):
    blocks = (4, 4, 2, 32, 256)
    hbm = pl.BlockSpec(memory_space=pl.ANY)
    vmem = pl.BlockSpec(memory_space=pltpu.VMEM)
    dma = pltpu.SemaphoreType.DMA
    gathered = jax.ShapeDtypeStruct((4, 4, 2, 32, 256), BF16)
    share = jax.ShapeDtypeStruct((32, 256), F32)
    small = jax.ShapeDtypeStruct((8, 128), BF16)
    slot = jax.ShapeDtypeStruct((1, 32), F32)
    shapes = (jax.ShapeDtypeStruct((256, 1024), BF16), gathered, gathered, gathered, small, small)
    shapes += (share,) * 4 + (slot,) * 2
    out = pl.pallas_call(
        kernel,
        out_shape=tuple(pltpu.VMEM(o.shape, o.dtype) for o in shapes),
        in_specs=[hbm] * 12,
        out_specs=(vmem,) * 12,
        scratch_shapes=[
            pltpu.VMEM((2, 2, *blocks), F32),
            pltpu.VMEM((256, 1024), F32),
            pltpu.VMEM((2, 2, 4, 2, 4, 32, 128), F32),
            pltpu.VMEM((2, 2, 4, 3, 2, 32, 128), BF16),
            pltpu.VMEM((2, 2, 4, 3, 2, 32, 128), BF16),
            pltpu.VMEM((2, 2, 3, 2, 32, 128), BF16),
            pltpu.VMEM((2, 2, 3, 2, 32, 128), BF16),
            pltpu.VMEM((2, 2, 2, 32, 128), F32),
            pltpu.VMEM((2, 2, 2, 4, 4, 2, 32, 128), BF16),
            pltpu.VMEM((4, 32, 256), F32),
            pltpu.VMEM((2, 8, 128), F32),
            pltpu.VMEM((2, 8, 128), F32),
            pltpu.VMEM((4, 2, 8, 128), F32),
            pltpu.VMEM((4, 2, 8, 128), F32),
            pltpu.VMEM((2, 1, 32), F32),
            dma((2, 4, 2)),
            dma((6,)),
            dma((4,)),
            dma((2, 2, 4)),
            dma((2, 2, 4)),
            dma((2, 2)),
            dma((2, 2, 3)),
            dma((2, 2, 3, 4)),
            dma((2, 2, 4, 4)),
            dma((6,)),
            dma((3,)),
            dma((3,)),
            pltpu.SemaphoreType.REGULAR,
        ],
        compiler_params=pltpu.CompilerParams(collective_id=0, has_side_effects=True, vmem_limit_bytes=60 * 2**20),
        name="step",
    )(
        pm[0], pq.reshape(blocks), pk.reshape(blocks), pv.reshape(blocks), pn.reshape(8, 128), pb.reshape(8, 128),
        mm.T, mq, mk, mv, mn.reshape(1, 32), mb.reshape(1, 32),
    )
    cm, cq, ck, cv, cn, cb, sm, sq, sk, sv, sn, sb = pl.pallas_call(
        placed,
        out_shape=shapes,
        in_specs=[vmem] * 12,
        out_specs=(hbm,) * 12,
        scratch_shapes=[dma((12,))],
        name="placed",
    )(*[pltpu.with_memory_space_constraint(o, pltpu.VMEM) for o in out])
    whole = (1024, 256)
    return (
        cq.reshape(whole), ck.reshape(whole), cv.reshape(whole), cm, cn.reshape(1024), cb.reshape(1024),
        sq, sk, sv, sm.T, sn.reshape(32), sb.reshape(32),
    )


def solution(mesh):
    in_specs = (
        P("batch", None, "cols"),
        P("batch", None, "cols"),
        P("batch", None, "cols"),
        P("batch", "cols", None),
        P("batch", None),
        P("batch", None),
        P("batch", "cols"),
        P("batch", "cols"),
        P("batch", "cols"),
        P("cols", "batch"),
        P("batch"),
        P("batch"),
    )
    out_specs = (
        P(None, "cols"),
        P(None, "cols"),
        P(None, "cols"),
        P("cols", None),
        P(),
        P(),
        P("batch", "cols"),
        P("batch", "cols"),
        P("batch", "cols"),
        P("cols", "batch"),
        P("batch"),
        P("batch"),
    )
    return jax.shard_map(per_device, mesh=mesh, in_specs=in_specs, out_specs=out_specs, check_vma=False)
```

time: 33.6 us -> 32.4 us (0.964)
  Pallas kernels: 32.9 us -> 31.6 us
    pallas_call x1, Pallas kernels: 31.4 us -> 30.1 us  [per_device(): pl.pallas_call(kernel, out_shape=tuple((pltpu.VMEM(o.shape, o.dtype) for...]
where the time goes in v4:
time: 32.4 us; the launch traced here: 32.3 us
  Pallas kernels  31.6 us (98%)
  between operations  0.66 us (2%)
    pallas_call x1, Pallas kernels, per_device(): pl.pallas_call(kernel, out_shape=tuple((pltpu.VMEM(o.shape, o.dtype) for...  30.1 us
    pallas_call x1, Pallas kernels, per_device(): pl.pallas_call(placed, out_shape=shapes, in_specs=[vmem] * 12, out_specs=...  1.47 us

profile of v4, /device:TPU:1, one launch (start us, length us, event | category | flops | bytes accessed | tf_op | source)
XLA Modules:
  0.0 32.3 jit_solution(8110747305452805566)
XLA Ops:
  0.6 30.1 %step.1 = (bf16[256,1024]{1,0:T(8,128)(2,1)S(1)}, bf16[4,4,2,32,256]{4,3,2,1,0:T(8,128)(2,1)S(1)}, bf16[4,4,2,32,256]{4,3,2,1,0:T(8,128)(2,1)S(1)}, bf16[4,4,2,3...) custom-call(f32[256,1024]{1,0:T(8,128)} %bitcast.17, ...), custom_call_target="tpu_custom_call" | custom-call | tf_op jit(solution)/shard_map/step/pallas_call | solution.py:348
  30.8 1.5 %placed.1 = (bf16[256,1024]{1,0:T(8,128)(2,1)}, bf16[4,4,2,32,256]{4,3,2,1,0:T(8,128)(2,1)}, bf16[4,4,2,32,256]{4,3,2,1,0:T(8,128)(2,1)}, bf16[4,4,2,32,256]{4,3...) custom-call(bf16[256,1024]{1,0:T(8,128)(2,1)S(1)} %get-tuple-element, ...), custom_call_target="tpu_custom_call" | custom-call | tf_op jit(solution)/shard_map/placed/pallas_call | solution.py:389

commit v5 on v4

--- a/solution.py
+++ b/solution.py
@@ -18,6 +18,7 @@
 SHIFT = 125.0
 PAIR_TOP = 2.6
 ORDER = (2, 1, 3, 0)
+LATE = ((1, 2), (1, 3))
 BACK = (1, 3, 2)
 FOUR_TOP = 10.4
 
@@ -50,7 +51,7 @@
     def at(z, x, core):
         return (z * 8 + x * 2 + core, col)
 
-    def ahead(axis, j):
+    def ahead(axis, j, core=core):
         return at(z, (x + j) % 4, core) if axis == 0 else at((z + j) % 4, x, core)
 
     def wait(ref, sem):
@@ -182,6 +183,8 @@
         part = gat.at[g, h, core, first[h], back(1, h, r)]
         for j in (2, 1, 3):
             remote(part, part, sent.at[4], g2r.at[g, h, j - 1, r], ahead(h, j))
+        for j in (2, 1, 3) if (g, r) in LATE else ():
+            remote(part, part, sent.at[5], fr.at[g, h, j, r], ahead(h, j, 1 - core))
 
     def hand_over(g, h, j, r):
         part = gat.at[g, h, core, back(0, h, j), back(1, h, r)]
@@ -209,7 +212,8 @@
 
     def g2(g, h, j, r):
         wait(gat.at[g, h, core, back(0, h, j), back(1, h, r)], g2r.at[g, h, j - 1, r])
-        hand_over(g, h, j, r)
+        if (g, r) not in LATE:
+            hand_over(g, h, j, r)
         place(g, h, core, j, r)
 
     def last(g, h, j, r):

time: 32.4 us -> 31.8 us (0.981)
  Pallas kernels: 31.6 us -> 31 us
    pallas_call x1, Pallas kernels: 30.1 us -> 29.5 us  [per_device(): pl.pallas_call(kernel, out_shape=tuple((pltpu.VMEM(o.shape, o.dtype) for...]
where the time goes in v5:
time: 31.8 us; the launch traced here: 31.6 us
  Pallas kernels  31 us (97%)
  between operations  0.66 us (2%)
    pallas_call x1, Pallas kernels, per_device(): pl.pallas_call(kernel, out_shape=tuple((pltpu.VMEM(o.shape, o.dtype) for...  29.5 us
    pallas_call x1, Pallas kernels, per_device(): pl.pallas_call(placed, out_shape=shapes, in_specs=[vmem] * 12, out_specs=...  1.47 us

profile of v5, /device:TPU:1, one launch (start us, length us, event | category | flops | bytes accessed | tf_op | source)
XLA Modules:
  0.0 31.6 jit_solution(6944742004901261299)
XLA Ops:
  0.6 29.5 %step.1 = (bf16[256,1024]{1,0:T(8,128)(2,1)S(1)}, bf16[4,4,2,32,256]{4,3,2,1,0:T(8,128)(2,1)S(1)}, bf16[4,4,2,32,256]{4,3,2,1,0:T(8,128)(2,1)S(1)}, bf16[4,4,2,3...) custom-call(f32[256,1024]{1,0:T(8,128)} %bitcast.17, ...), custom_call_target="tpu_custom_call" | custom-call | tf_op jit(solution)/shard_map/step/pallas_call | solution.py:352
  30.2 1.5 %placed.1 = (bf16[256,1024]{1,0:T(8,128)(2,1)}, bf16[4,4,2,32,256]{4,3,2,1,0:T(8,128)(2,1)}, bf16[4,4,2,32,256]{4,3,2,1,0:T(8,128)(2,1)}, bf16[4,4,2,32,256]{4,3...) custom-call(bf16[256,1024]{1,0:T(8,128)(2,1)S(1)} %get-tuple-element, ...), custom_call_target="tpu_custom_call" | custom-call | tf_op jit(solution)/shard_map/placed/pallas_call | solution.py:393

commit v6 on v5

--- a/solution.py
+++ b/solution.py
@@ -13,8 +13,8 @@
 
 RATE = 0.4 * 32**-0.5
 
-SPREAD = 21.0
-STEPS = 4096.0
+SPREAD = 15.75
+STEPS = 65536.0
 SHIFT = 125.0
 PAIR_TOP = 2.6
 ORDER = (2, 1, 3, 0)
@@ -284,12 +284,10 @@
         pl.semaphore_wait(hands, 1)
 
     over(e1, 0, 2)
+    over(e1, 0, 1)
     turned.wait()
-    turn(0)
-    turn(1)
-    over(e1, 0, 1)
-    turn(2)
-    turn(3)
+    for c in range(4):
+        turn(c)
     value.wait()
     over(share, 1, *ORDER)
     over(e1, 0, 3, 0)
@@ -298,9 +296,10 @@
     over(r1, 0, *ORDER)
     for copy in masters:
         copy.wait()
-    over(r1, 1, *ORDER)
+    over(r1, 1, 2, 1, 3)
     over(r2, 0, ())
     over(own, 0, ())
+    over(r1, 1, 0)
     n2()
     over(r2, 1, ())
     over(own, 1, ())

time: 31.8 us -> 31.7 us (level)
  no operation moved by 1% of the time
where the time goes in v6:
time: 31.7 us; the launch traced here: 31.6 us
  Pallas kernels  30.9 us (97%)
  between operations  0.66 us (2%)
    pallas_call x1, Pallas kernels, per_device(): pl.pallas_call(kernel, out_shape=tuple((pltpu.VMEM(o.shape, o.dtype) for...  29.4 us
    pallas_call x1, Pallas kernels, per_device(): pl.pallas_call(placed, out_shape=shapes, in_specs=[vmem] * 12, out_specs=...  1.47 us

profile of v6, /device:TPU:1, one launch (start us, length us, event | category | flops | bytes accessed | tf_op | source)
XLA Modules:
  0.0 31.6 jit_solution(15168784187456183410)
XLA Ops:
  0.6 29.4 %step.1 = (bf16[256,1024]{1,0:T(8,128)(2,1)S(1)}, bf16[4,4,2,32,256]{4,3,2,1,0:T(8,128)(2,1)S(1)}, bf16[4,4,2,32,256]{4,3,2,1,0:T(8,128)(2,1)S(1)}, bf16[4,4,2,3...) custom-call(f32[256,1024]{1,0:T(8,128)} %bitcast.17, ...), custom_call_target="tpu_custom_call" | custom-call | tf_op jit(solution)/shard_map/step/pallas_call | solution.py:351
  30.1 1.5 %placed.1 = (bf16[256,1024]{1,0:T(8,128)(2,1)}, bf16[4,4,2,32,256]{4,3,2,1,0:T(8,128)(2,1)}, bf16[4,4,2,32,256]{4,3,2,1,0:T(8,128)(2,1)}, bf16[4,4,2,32,256]{4,3...) custom-call(bf16[256,1024]{1,0:T(8,128)(2,1)S(1)} %get-tuple-element, ...), custom_call_target="tpu_custom_call" | custom-call | tf_op jit(solution)/shard_map/placed/pallas_call | solution.py:392

commit v7 on v6

--- a/solution.py
+++ b/solution.py
@@ -122,16 +122,6 @@
                 loads[h, r, i].wait()
             share(0, h, r)
 
-    for copy in small:
-        copy.wait()
-    lanes = lax.broadcasted_iota(jnp.int32, (8, 128), 1)
-    rows = lax.broadcasted_iota(jnp.int32, (8, 128), 0)
-    mine = (rows * 4 + lanes // 32) == b
-    for i in range(2):
-        m = jnp.concatenate([nmast[i]] * 4, axis=1)
-        nbuf[i] = jnp.where(mine, jnp.broadcast_to(m, (8, 128)), 0.0) - RATE * nbuf[i]
-    remote(nbuf, npair, ns.at[0], nr.at[0], partner)
-
     def turn(c):
         raw[1, 0, c] = flat[:, 256 * c : 256 * c + 256].T.reshape(4, 2, 32, 256)
 
@@ -284,6 +274,15 @@
         pl.semaphore_wait(hands, 1)
 
     over(e1, 0, 2)
+    for copy in small:
+        copy.wait()
+    lanes = lax.broadcasted_iota(jnp.int32, (8, 128), 1)
+    rows = lax.broadcasted_iota(jnp.int32, (8, 128), 0)
+    mine = (rows * 4 + lanes // 32) == b
+    for i in range(2):
+        m = jnp.concatenate([nmast[i]] * 4, axis=1)
+        nbuf[i] = jnp.where(mine, jnp.broadcast_to(m, (8, 128)), 0.0) - RATE * nbuf[i]
+    remote(nbuf, npair, ns.at[0], nr.at[0], partner)
     over(e1, 0, 1)
     turned.wait()
     for c in range(4):

time: 31.7 us -> 31.5 us (level)
  no operation moved by 1% of the time
where the time goes in v7:
time: 31.5 us; the launch traced here: 31.4 us
  Pallas kernels  30.7 us (97%)
  between operations  0.66 us (2%)
    pallas_call x1, Pallas kernels, per_device(): pl.pallas_call(kernel, out_shape=tuple((pltpu.VMEM(o.shape, o.dtype) for...  29.3 us
    pallas_call x1, Pallas kernels, per_device(): pl.pallas_call(placed, out_shape=shapes, in_specs=[vmem] * 12, out_specs=...  1.47 us

profile of v7, /device:TPU:1, one launch (start us, length us, event | category | flops | bytes accessed | tf_op | source)
XLA Modules:
  0.0 31.4 jit_solution(3094700561613059765)
XLA Ops:
  0.6 29.3 %step.1 = (bf16[256,1024]{1,0:T(8,128)(2,1)S(1)}, bf16[4,4,2,32,256]{4,3,2,1,0:T(8,128)(2,1)S(1)}, bf16[4,4,2,32,256]{4,3,2,1,0:T(8,128)(2,1)S(1)}, bf16[4,4,2,3...) custom-call(f32[256,1024]{1,0:T(8,128)} %bitcast.17, ...), custom_call_target="tpu_custom_call" | custom-call | tf_op jit(solution)/shard_map/step/pallas_call | solution.py:350
  29.9 1.5 %placed.1 = (bf16[256,1024]{1,0:T(8,128)(2,1)}, bf16[4,4,2,32,256]{4,3,2,1,0:T(8,128)(2,1)}, bf16[4,4,2,32,256]{4,3,2,1,0:T(8,128)(2,1)}, bf16[4,4,2,32,256]{4,3...) custom-call(bf16[256,1024]{1,0:T(8,128)(2,1)S(1)} %get-tuple-element, ...), custom_call_target="tpu_custom_call" | custom-call | tf_op jit(solution)/shard_map/placed/pallas_call | solution.py:391
